TPU v7x, 32 devices: a whole 2x2x4 slice. The times are simulated.
32 devices in a mesh: panel: 16 (over z, y, x), lag: 2 (over core).
Axes of the slice: x: 2, y: 2, z: 4, core: 2. Of those that a mesh axis runs over, the one named last changes fastest.
Arguments:
- history: bfloat16 [2, 32, 512, 128], P('lag', 'panel'), may hold values from -6 to 6
- weights: bfloat16 [16, 2, 6, 512, 512], P('panel', 'lag'), may hold values from -0.25 to 0.25
- pairs: int32 [16, 2, 6, 3], P('panel', 'lag'), may hold values from 0 to 4, as said below
- counts: int32 [16, 2], P('panel', 'lag'), may hold values from 3 to 6, as said below
- send_list: int32 [16, 2, 5, 2], P(None, 'lag'), may hold values from 0 to 1
- incident: bfloat16 [32, 512, 128], P(('panel', 'lag')), may hold values from -6 to 6
- near_inverse: bfloat16 [32, 512, 512], P(('panel', 'lag')), may hold values from -0.25 to 0.25
Outputs:
- density: bfloat16 [32, 512, 128], P(('panel', 'lag'))
Inputs may be any that keep to these rules, and one draw needn't show every extreme that they name: pairs[p, g, k] = (o, c, r) with o in 0 to 4, c in 0 to 1, r in 0 to 1; the (o, c) of one device's pairs are distinct. `counts`: panel index 0 at lag index 0 has 6 pairs.
All inputs are finite; a program needn't handle non-finite values.
Results may differ from a plain program's by a relative error of at most 0.0083.
Values may be sent and summed in bfloat16 or wider, within the bound.
A program may use at most 64 MiB of HBM per device.

v0:
```python
import functools

import jax
import jax.numpy as jnp
from jax import lax
from jax.experimental import pallas as pl
from jax.experimental.pallas import tpu as pltpu
from jax.sharding import PartitionSpec as P

CHUNKS = 2
PARTS = 4


def step_kernel(
    relay, panels, lags,
    pairs_ref, counts_ref, send_ref, local_ref, weights_ref, incident_ref, near_ref,
    out_ref,
    windows, weights, near, incident, right, running, partial_value, landed,
    send_sem, recv_sem, local_sem, weight_sem, near_sem, incident_sem,
    sum_send_sem, sum_recv_sem,
):
    here = lax.axis_index("panel")
    lag = lax.axis_index("lag")
    offsets = send_ref.shape[1]
    reach = offsets // 2
    blocks, piece, fields = windows[0].shape[1:]
    depth = piece * PARTS
    count = weights.shape[0]
    own = incident.shape[0]
    side = 2 * lax.rem(here, 2) - 1

    def panel(steps):
        return lax.rem(here + steps + panels, panels)

    def rows_of(part):
        return pl.ds(part * piece, piece)

    def outgoing(steps, part):
        if relay:
            return windows[part].at[0]
        return local_ref.at[reach - steps, :, rows_of(part)]

    source_here = local_ref.at[0] if relay else local_ref.at[reach]
    locals_here = [
        pltpu.make_async_copy(
            source_here.at[:, rows_of(part)], windows[part].at[0], local_sem.at[part]
        )
        for part in range(PARTS)
    ]
    for copy in locals_here:
        copy.start()
    weight_copies = [
        pltpu.make_async_copy(weights_ref.at[0, 0, k], weights.at[k], weight_sem.at[k])
        for k in range(count)
    ]

    barrier = pltpu.get_barrier_semaphore()
    greeted = [-side, 2 * side, -2 * side] + ([] if relay else [side])
    for steps in greeted:
        pl.semaphore_signal(
            barrier, inc=1, device_id={"panel": panel(steps)},
            device_id_type=pl.DeviceIdType.MESH,
        )
    for ahead in range(1, lags):
        pl.semaphore_signal(
            barrier, inc=1, device_id={"lag": lax.rem(lag + ahead, lags)},
            device_id_type=pl.DeviceIdType.MESH,
        )
    pl.semaphore_wait(barrier, len(greeted) + lags - 1)
    for copy in locals_here:
        copy.wait()

    def send(source, slot, part, steps):
        copy = pltpu.make_async_remote_copy(
            src_ref=source,
            dst_ref=windows[part].at[slot],
            send_sem=send_sem.at[slot - 1, part],
            recv_sem=recv_sem.at[slot - 1, part],
            device_id={"panel": panel(steps)},
            device_id_type=pl.DeviceIdType.MESH,
        )
        copy.start()
        return copy

    first, second, partner, passed = [], [], [], []
    lead = PARTS // 2
    for step in range(PARTS + lead):
        if step < PARTS:
            first.append(send(outgoing(2 * side, step), 3, step, 2 * side))
            partner.append(send(outgoing(-side, step), 4, step, -side))
        if step >= lead:
            part = step - lead
            second.append(send(outgoing(-2 * side, part), 2, part, -2 * side))
    near_copy = pltpu.make_async_copy(near_ref, near, near_sem)
    incident_copy = pltpu.make_async_copy(incident_ref, incident, incident_sem)
    for copy in weight_copies:
        copy.start()
    incident_copy.start()
    near_copy.start()
    def pass_on(part):
        if relay:
            first[part].wait_recv()
            passed.append(send(windows[part].at[3], 1, part, -side))
        else:
            passed.append(send(outgoing(side, part), 1, part, side))

    for part in range(PARTS):
        pass_on(part)
    for copy in weight_copies:
        copy.wait()
    incident_copy.wait()
    near_copy.wait()

    live = counts_ref[0, 0]
    readers = right.shape[2] // fields
    chosen = []
    for k in range(count):
        offset = pairs_ref[0, 0, 0, k]
        slot = pairs_ref[0, 1, 0, k]
        reader = pairs_ref[0, 2, 0, k]
        if relay:
            block = send_ref[0, offset, slot, panel(offset - reach)]
        else:
            block = slot
        place = lax.rem((offset - reach) * side + offsets, offsets)
        chosen.append((place, block, reader))

    def arrive(part):
        if not relay:
            first[part].wait_recv()
        partner[part].wait_recv()
        second[part].wait_recv()
        passed[part].wait_recv()
        for k, (place, block, reader) in enumerate(chosen):
            value = windows[part][place, block]
            for r in range(readers):
                kept = jnp.logical_and(reader == r, k < live)
                right[part, k * piece:(k + 1) * piece, r * fields:(r + 1) * fields] = jnp.where(
                    kept, value, jnp.zeros_like(value)
                )

    def product(part, at):
        left = jnp.concatenate(
            [weights[k, at, part * piece:(part + 1) * piece] for k in range(count)], axis=1
        )
        return jnp.dot(left, right[part], preferred_element_type=jnp.float32)

    rows = depth // CHUNKS
    sums = []
    for part in range(PARTS - 1):
        arrive(part)
        for chunk in range(CHUNKS):
            at = slice(chunk * rows, (chunk + 1) * rows)
            term = product(part, at)
            running[at, :] = term if part == 0 else running[at, :] + term
    arrive(PARTS - 1)
    for chunk in range(CHUNKS):
        at = slice(chunk * rows, (chunk + 1) * rows)
        total = running[at, :] + product(PARTS - 1, at)
        for r in range(readers):
            partial_value[r, at, :] = total[:, r * fields:(r + 1) * fields]
        for ahead in range(1, lags):
            other = lax.rem(lag + ahead, lags)
            copy = pltpu.make_async_remote_copy(
                src_ref=partial_value.at[pl.ds(other * own, own), pl.ds(chunk * rows, rows)],
                dst_ref=landed.at[ahead - 1, :, pl.ds(chunk * rows, rows)],
                send_sem=sum_send_sem.at[ahead - 1, chunk],
                recv_sem=sum_recv_sem.at[ahead - 1, chunk],
                device_id={"lag": other},
                device_id_type=pl.DeviceIdType.MESH,
            )
            copy.start()
            sums.append(copy)
    for copy in first + partner + second + passed:
        copy.wait_send()
    for copy in sums:
        copy.wait_recv()
    for j in range(own):
        summed = partial_value[lag * own + j]
        for ahead in range(1, lags):
            summed = summed + landed[ahead - 1, j]
        remainder = (incident[j].astype(jnp.float32) - summed).astype(jnp.bfloat16)
        out_ref[j] = jnp.dot(
            near[j], remainder, preferred_element_type=jnp.float32
        ).astype(out_ref.dtype)
    for copy in sums:
        copy.wait_send()


def on_device(panels, lags, history, weights, pairs, counts, send_list, incident, near_inverse):
    readers, depth, fields = history.shape[1:]
    offsets, slots = send_list.shape[2:]
    assert offsets == 5 and panels % 2 == 0 and panels > offsets
    count = weights.shape[2]
    own = incident.shape[0]
    relay = readers <= slots
    blocks = readers if relay else slots
    local = history
    if not relay:
        here = lax.axis_index("panel")
        mine = lax.dynamic_index_in_dim(send_list, here, 0, keepdims=False)[0]
        local = jnp.take(history[0], mine.reshape(-1), axis=0).reshape(
            (offsets, slots, depth, fields)
        )
    anywhere = pl.BlockSpec(memory_space=pl.ANY)
    scalars = pl.BlockSpec(memory_space=pltpu.SMEM)
    dma = pltpu.SemaphoreType.DMA
    return pl.pallas_call(
        functools.partial(step_kernel, relay, panels, lags),
        out_shape=jax.ShapeDtypeStruct(incident.shape, jnp.bfloat16),
        in_specs=[scalars] * 3 + [anywhere] * 4,
        out_specs=pl.BlockSpec(memory_space=pltpu.VMEM),
        scratch_shapes=[
            [pltpu.VMEM((offsets, blocks, depth // PARTS, fields), history.dtype)] * PARTS,
            pltpu.VMEM(weights.shape[2:], weights.dtype),
            pltpu.VMEM(near_inverse.shape, near_inverse.dtype),
            pltpu.VMEM(incident.shape, incident.dtype),
            pltpu.VMEM((PARTS, count * depth // PARTS, readers * fields), history.dtype),
            pltpu.VMEM((depth, readers * fields), jnp.float32),
            pltpu.VMEM((readers, depth, fields), jnp.float32),
            pltpu.VMEM((lags - 1, own, depth, fields), jnp.float32),
            dma((offsets - 1, PARTS)),
            dma((offsets - 1, PARTS)),
            dma((PARTS,)),
            dma((count,)),
            dma,
            dma,
            dma((lags - 1, CHUNKS)),
            dma((lags - 1, CHUNKS)),
        ],
        compiler_params=pltpu.CompilerParams(
            collective_id=0, has_side_effects=True, vmem_limit_bytes=67043328
        ),
    )(jnp.transpose(pairs, (0, 3, 1, 2)), counts, jnp.transpose(send_list, (1, 2, 3, 0)), local, weights, incident, near_inverse)


def solution(mesh):
    return jax.shard_map(
        functools.partial(on_device, mesh.shape["panel"], mesh.shape["lag"]),
        mesh=mesh,
        in_specs=(
            P("lag", "panel", None, None),
            P("panel", "lag", None, None, None),
            P("panel", "lag", None, None),
            P("panel", "lag"),
            P(None, "lag", None, None),
            P(("panel", "lag"), None, None),
            P(("panel", "lag"), None, None),
        ),
        out_specs=P(("panel", "lag"), None, None),
        check_vma=False,
    )
```

profile of v0, /device:TPU:1, one launch (start us, length us, event | category | flops | bytes accessed | tf_op | source)
XLA Modules:
  0.0 25.1 jit_solution(16846245785064019495)
XLA Ops:
  0.7 22.9 %shard_map.73 = bf16[1,512,128]{2,1,0:T(8,128)(2,1)} custom-call(s32[1,3,1,6]{3,2,1,0:T(1,128)} %bitcast.3, s32[1,1]{1,0:T(1,128)S(6)} %copy.9.counts_ref, s32[1,5,2,16]{3,2,1,0:T(2,128)} %bitcast.2, bf16[1,2,512,128]{3,2,1,0:T(8,128)(2,1)} %local_ref.1, bf16[1,1,6,512,512]{4,3,2,1,0:T(8,128)(2,1)} %weights_ref.1, bf16[1,512,128]{2,1,0:T(8,128)(2,1)} %incident_ref.1, ...), custom_call_target="tpu_custom_call" | custom-call | tf_op jit(solution)/shard_map/pallas_call | solution.py:208
  23.6 1.6 %copy.10 = bf16[1,512,128]{2,1,0:T(8,128)(2,1)} copy(bf16[1,512,128]{2,1,0:T(8,128)(2,1)} %shard_map.73) | data formatting | bytes 262144
where the time goes:
time: 25.3 us; the launch traced here: 25.1 us
  Pallas kernels  22.9 us (91%)
  local copies, waits for them, and re-layouts  1.57 us (6%)
  between operations  0.66 us (3%)
    pallas_call x1, Pallas kernels, on_device(): pl.pallas_call(functools.partial(step_kernel, relay, panels, lags), out_s...  22.9 us
    unnamed x1, local copies, waits for them, and re-layouts  1.57 us

commit v1 on v0

--- a/solution.py
+++ b/solution.py
@@ -9,6 +9,336 @@
 
 CHUNKS = 2
 PARTS = 4
+
+NEAR_BY_X = 2
+FAR_BY_X = 3
+ORDER = (0, 3, 1, 2)
+OWN, ACROSS, BESIDE, BEYOND, FOURTH, TRANSIT = range(6)
+
+
+def relay_kernel(
+    panels, lags,
+    counts_ref, pairs_hbm, send_hbm, local_ref, weights_ref, incident_ref, near_ref,
+    out_ref,
+    pairs_ref, send_ref, scalar_sem,
+    windows, weights, near, incident, right, running, partial_value, landed,
+    send_sem, recv_sem, local_sem, weight_sem, near_sem, incident_sem,
+    sum_send_sem, sum_recv_sem, chain_sem,
+):
+    here = lax.axis_index("panel")
+    lag = lax.axis_index("lag")
+    offsets = send_ref.shape[1]
+    reach = offsets // 2
+    blocks, piece, fields = windows[0].shape[1:]
+    depth = piece * PARTS
+    count = weights.shape[0]
+    own = incident.shape[0]
+    places = panels // 4
+    x = lax.rem(here, 2)
+    y = lax.rem(here // 2, 2)
+    way = 1 - 2 * y
+    z = here // 4
+    at_chain = jnp.where(y == 0, z, places - 1 - z)
+    feeds_near = x == y
+
+    def panel(steps):
+        return lax.rem(here + steps + panels, panels)
+
+    to_x = panel(1 - 2 * x)
+    to_y = panel(2 * way)
+    to_z = panel(4 * way)
+    from_z = panel(-4 * way)
+
+    def rows_of(part):
+        return pl.ds(part * piece, piece)
+
+    locals_here = [
+        pltpu.make_async_copy(
+            local_ref.at[0, :, rows_of(part)], windows[part].at[OWN], local_sem.at[part]
+        )
+        for part in range(PARTS)
+    ]
+    for copy in locals_here:
+        copy.start()
+    scalar_copies = [
+        pltpu.make_async_copy(source, target, scalar_sem.at[i])
+        for i, (source, target) in enumerate(
+            [(pairs_hbm, pairs_ref), (send_hbm, send_ref)]
+        )
+    ]
+    for copy in scalar_copies:
+        copy.start()
+    weight_copies = [
+        pltpu.make_async_copy(weights_ref.at[0, 0, k], weights.at[k], weight_sem.at[k])
+        for k in range(count)
+    ]
+
+    barrier = pltpu.get_barrier_semaphore()
+
+    def greet(semaphore, **device):
+        pl.semaphore_signal(
+            semaphore, inc=1, device_id=device, device_id_type=pl.DeviceIdType.MESH
+        )
+
+    greet(barrier, panel=to_x)
+    greet(barrier, panel=to_y)
+
+    @pl.when(at_chain > 0)
+    def _():
+        greet(barrier, panel=from_z)
+
+    for ahead in range(1, lags):
+        greet(barrier, lag=lax.rem(lag + ahead, lags))
+    pl.semaphore_wait(
+        barrier, 2 + lags - 1 + jnp.where(at_chain < places - 1, 1, 0).astype(jnp.int32)
+    )
+    for copy in locals_here:
+        copy.wait()
+
+    def copy_of(source, target, link, part, block, device):
+        return pltpu.make_async_remote_copy(
+            src_ref=windows[part].at[source, block],
+            dst_ref=windows[part].at[target, block],
+            send_sem=send_sem.at[link, part, block],
+            recv_sem=recv_sem.at[target - 1, part, block],
+            device_id={"panel": device},
+            device_id_type=pl.DeviceIdType.MESH,
+        )
+
+    def by_x(part, block):
+        return copy_of(OWN, ACROSS, 0, part, block, to_x)
+
+    def by_y(part, block):
+        return copy_of(OWN, BESIDE, 1, part, block, to_y)
+
+    def by_z(part, block):
+        return copy_of(BESIDE, BEYOND, 2, part, block, to_z)
+
+    def fourth_by_x(part, block):
+        return copy_of(jnp.where(feeds_near, BESIDE, BEYOND), FOURTH, 3, part, block, to_x)
+
+    def fourth_by_y(part, block):
+        return copy_of(
+            ACROSS, jnp.where(feeds_near, FOURTH, TRANSIT), 4, part, block, to_y
+        )
+
+    def fourth_by_z(part, block):
+        return copy_of(TRANSIT, FOURTH, 5, part, block, to_z)
+
+    def landing(slot, part, block):
+        return copy_of(slot, slot, 0, part, block, to_x)
+
+    pieces = [(part, block) for part in range(PARTS) for block in range(blocks)]
+    backward = pieces[::-1]
+    for one, other in zip(backward, pieces):
+        by_x(*one).start()
+        by_y(*other).start()
+
+    @pl.when(at_chain > 0)
+    def _():
+        pl.semaphore_wait(chain_sem, 1)
+
+    @pl.when(at_chain < places - 1)
+    def _():
+        greet(chain_sem, panel=to_z)
+
+    near_copy = pltpu.make_async_copy(near_ref, near, near_sem)
+    incident_copy = pltpu.make_async_copy(incident_ref, incident, incident_sem)
+    for copy in weight_copies:
+        copy.start()
+    incident_copy.start()
+    near_copy.start()
+
+    behind = 3
+    total_steps = len(pieces) + behind
+    for step in range(total_steps):
+        if step < len(pieces):
+            part, block = backward[step]
+            landing(ACROSS, part, block).wait_recv()
+            if part >= max(NEAR_BY_X, FAR_BY_X):
+                fourth_by_y(part, block).start()
+            elif part >= NEAR_BY_X:
+                @pl.when(feeds_near)
+                def _():
+                    fourth_by_y(part, block).start()
+            elif part >= FAR_BY_X:
+                @pl.when(jnp.logical_not(feeds_near))
+                def _():
+                    fourth_by_y(part, block).start()
+            part, block = pieces[step]
+            landing(BESIDE, part, block).wait_recv()
+            by_z(part, block).start()
+            if part < NEAR_BY_X:
+                @pl.when(feeds_near)
+                def _():
+                    fourth_by_x(part, block).start()
+        if step >= behind:
+            part, block = pieces[step - behind]
+
+            @pl.when(jnp.logical_not(feeds_near))
+            def _():
+                landing(BEYOND, part, block).wait_recv()
+                if part < FAR_BY_X:
+                    fourth_by_x(part, block).start()
+
+    @pl.when(feeds_near)
+    def _():
+        for part, block in backward:
+            if part >= FAR_BY_X:
+                landing(TRANSIT, part, block).wait_recv()
+                fourth_by_z(part, block).start()
+        for part, block in pieces:
+            landing(BEYOND, part, block).wait_recv()
+
+    for copy in scalar_copies + weight_copies:
+        copy.wait()
+    incident_copy.wait()
+    near_copy.wait()
+
+    live = counts_ref[0, 0]
+    readers = right.shape[2] // fields
+    chosen = []
+    for k in range(count):
+        offset = pairs_ref[0, 0, 0, k]
+        slot = pairs_ref[0, 1, 0, k]
+        reader = pairs_ref[0, 2, 0, k]
+        steps = offset - reach
+        block = send_ref[0, offset, slot, panel(steps)]
+        place = jnp.where(
+            steps == 0, OWN,
+            jnp.where(
+                steps == 1 - 2 * x, ACROSS,
+                jnp.where(
+                    steps == 2 * way, BESIDE, jnp.where(steps == -2 * way, BEYOND, FOURTH)
+                ),
+            ),
+        )
+        chosen.append((place, block, reader))
+
+    def arrive(part):
+        for block in range(blocks):
+            landing(FOURTH, part, block).wait_recv()
+        for k, (place, block, reader) in enumerate(chosen):
+            value = windows[part][place, block]
+            for r in range(readers):
+                kept = jnp.logical_and(reader == r, k < live)
+                right[part, k * piece:(k + 1) * piece, r * fields:(r + 1) * fields] = jnp.where(
+                    kept, value, jnp.zeros_like(value)
+                )
+
+    def product(part, at):
+        left = jnp.concatenate(
+            [weights[k, at, part * piece:(part + 1) * piece] for k in range(count)], axis=1
+        )
+        return jnp.dot(left, right[part], preferred_element_type=jnp.float32)
+
+    rows = depth // CHUNKS
+    sums = []
+    for part in ORDER[:-1]:
+        arrive(part)
+        for chunk in range(CHUNKS):
+            at = slice(chunk * rows, (chunk + 1) * rows)
+            term = product(part, at)
+            running[at, :] = term if part == ORDER[0] else running[at, :] + term
+    arrive(ORDER[-1])
+    for chunk in range(CHUNKS):
+        at = slice(chunk * rows, (chunk + 1) * rows)
+        total = running[at, :] + product(ORDER[-1], at)
+        for r in range(readers):
+            partial_value[r, at, :] = total[:, r * fields:(r + 1) * fields]
+        for ahead in range(1, lags):
+            other = lax.rem(lag + ahead, lags)
+            copy = pltpu.make_async_remote_copy(
+                src_ref=partial_value.at[pl.ds(other * own, own), pl.ds(chunk * rows, rows)],
+                dst_ref=landed.at[ahead - 1, :, pl.ds(chunk * rows, rows)],
+                send_sem=sum_send_sem.at[ahead - 1, chunk],
+                recv_sem=sum_recv_sem.at[ahead - 1, chunk],
+                device_id={"lag": other},
+                device_id_type=pl.DeviceIdType.MESH,
+            )
+            copy.start()
+            sums.append(copy)
+    for part, block in pieces:
+        by_x(part, block).wait_send()
+        by_y(part, block).wait_send()
+        by_z(part, block).wait_send()
+
+    @pl.when(feeds_near)
+    def _():
+        for part, block in pieces:
+            if part < NEAR_BY_X:
+                fourth_by_x(part, block).wait_send()
+            else:
+                fourth_by_y(part, block).wait_send()
+            if part >= FAR_BY_X:
+                fourth_by_z(part, block).wait_send()
+
+    @pl.when(jnp.logical_not(feeds_near))
+    def _():
+        for part, block in pieces:
+            if part < FAR_BY_X:
+                fourth_by_x(part, block).wait_send()
+            else:
+                fourth_by_y(part, block).wait_send()
+
+    for copy in sums:
+        copy.wait_recv()
+    for j in range(own):
+        summed = partial_value[lag * own + j]
+        for ahead in range(1, lags):
+            summed = summed + landed[ahead - 1, j]
+        remainder = (incident[j].astype(jnp.float32) - summed).astype(jnp.bfloat16)
+        out_ref[j] = jnp.dot(
+            near[j], remainder, preferred_element_type=jnp.float32
+        ).astype(out_ref.dtype)
+    for copy in sums:
+        copy.wait_send()
+
+
+def relayed(panels, lags, history, weights, pairs, counts, send_list, incident, near_inverse):
+    readers, depth, fields = history.shape[1:]
+    count = weights.shape[2]
+    own = incident.shape[0]
+    piece = depth // PARTS
+    in_hbm = pl.BlockSpec(memory_space=pltpu.HBM)
+    dma = pltpu.SemaphoreType.DMA
+    held = [
+        pltpu.with_memory_space_constraint(operand, pltpu.HBM)
+        for operand in (
+            jnp.transpose(pairs, (0, 3, 1, 2)), jnp.transpose(send_list, (1, 2, 3, 0)),
+            history, weights, incident, near_inverse,
+        )
+    ]
+    return pl.pallas_call(
+        functools.partial(relay_kernel, panels, lags),
+        out_shape=pltpu.VMEM(incident.shape, jnp.bfloat16),
+        in_specs=[pl.BlockSpec(memory_space=pltpu.SMEM)] + [in_hbm] * 6,
+        out_specs=pl.BlockSpec(memory_space=pltpu.VMEM),
+        scratch_shapes=[
+            *[pltpu.SMEM(operand.shape, operand.dtype) for operand in held[:2]],
+            dma((2,)),
+            [pltpu.VMEM((TRANSIT + 1, readers, piece, fields), history.dtype)] * PARTS,
+            pltpu.VMEM(weights.shape[2:], weights.dtype),
+            pltpu.VMEM(near_inverse.shape, near_inverse.dtype),
+            pltpu.VMEM(incident.shape, incident.dtype),
+            pltpu.VMEM((PARTS, count * piece, readers * fields), history.dtype),
+            pltpu.VMEM((depth, readers * fields), jnp.float32),
+            pltpu.VMEM((readers, depth, fields), jnp.float32),
+            pltpu.VMEM((lags - 1, own, depth, fields), jnp.float32),
+            dma((6, PARTS, readers)),
+            dma((TRANSIT, PARTS, readers)),
+            dma((PARTS,)),
+            dma((count,)),
+            dma,
+            dma,
+            dma((lags - 1, CHUNKS)),
+            dma((lags - 1, CHUNKS)),
+            pltpu.SemaphoreType.REGULAR,
+        ],
+        compiler_params=pltpu.CompilerParams(
+            collective_id=0, has_side_effects=True, vmem_limit_bytes=48 * 1024 * 1024
+        ),
+    )(counts, *held)
 
 
 def step_kernel(
@@ -193,6 +523,10 @@
     assert offsets == 5 and panels % 2 == 0 and panels > offsets
     count = weights.shape[2]
     own = incident.shape[0]
+    if readers <= slots and panels % 4 == 0 and panels > 8:
+        return relayed(
+            panels, lags, history, weights, pairs, counts, send_list, incident, near_inverse
+        )
     relay = readers <= slots
     blocks = readers if relay else slots
     local = history

time: 25.3 us -> 22.9 us (0.905)
  Pallas kernels: 22.9 us -> 21.4 us
  local copies, waits for them, and re-layouts: 1.57 us -> 0.66 us
    pallas_call x1, Pallas kernels: 22.9 us -> 21.4 us  [relayed(): pl.pallas_call(functools.partial(relay_kernel, panels, lags), out_shape=p...]
    unnamed x1, local copies, waits for them, and re-layouts: 1.57 us -> 0.66 us
where the time goes in v1:
time: 22.9 us; the launch traced here: 22.7 us
  Pallas kernels  21.4 us (93%)
  local copies, waits for them, and re-layouts  0.66 us (3%)
  between operations  0.66 us (3%)
    pallas_call x1, Pallas kernels, relayed(): pl.pallas_call(functools.partial(relay_kernel, panels, lags), out_shape=p...  21.4 us
    unnamed x1, local copies, waits for them, and re-layouts  0.66 us

profile of v1, /device:TPU:1, one launch (start us, length us, event | category | flops | bytes accessed | tf_op | source)
XLA Modules:
  0.0 22.7 jit_solution(1089946238324544334)
XLA Ops:
  0.7 21.4 %shard_map.73 = bf16[1,512,128]{2,1,0:T(8,128)(2,1)S(1)} custom-call(s32[1,1]{1,0:T(1,128)S(6)} %copy.10.counts_ref, s32[1,3,1,6]{3,2,1,0:T(1,128)} %bitcast.3, s32[1,5,2,16]{3,2,1,0:T(2,128)} %bitcast.2, bf16[1,2,512,128]{3,2,1,0:T(8,128)(2,1)} %local_ref.1, bf16[1,1,6,512,512]{4,3,2,1,0:T(8,128)(2,1)} %weights_ref.1, bf16[1,512,128]{2,1,0:T(8,128)(2,1)} %incident_ref.1, ...), custom_call_target="tpu_custom_call" | custom-call | tf_op jit(solution)/shard_map/pallas_call | solution.py:312
  22.0 0.7 %copy.9 = bf16[1,512,128]{2,1,0:T(8,128)(2,1)} copy(bf16[1,512,128]{2,1,0:T(8,128)(2,1)S(1)} %shard_map.73) | data formatting | bytes 262144

commit v2 on v1

--- a/solution.py
+++ b/solution.py
@@ -12,8 +12,12 @@
 
 NEAR_BY_X = 2
 FAR_BY_X = 3
-ORDER = (0, 3, 1, 2)
+RING_OWN = 1
+DIRECT = 2
 OWN, ACROSS, BESIDE, BEYOND, FOURTH, TRANSIT = range(6)
+BEHIND = 5
+ASIDE = 3
+LATE_GREETING = 3
 
 
 def relay_kernel(
@@ -21,13 +25,13 @@
     counts_ref, pairs_hbm, send_hbm, local_ref, weights_ref, incident_ref, near_ref,
     out_ref,
     pairs_ref, send_ref, scalar_sem,
-    windows, weights, near, incident, right, running, partial_value, landed,
+    windows, weights, near, incident, running, partial_value, landed,
     send_sem, recv_sem, local_sem, weight_sem, near_sem, incident_sem,
     sum_send_sem, sum_recv_sem, chain_sem,
 ):
     here = lax.axis_index("panel")
     lag = lax.axis_index("lag")
-    offsets = send_ref.shape[1]
+    offsets, slots = send_ref.shape[1:3]
     reach = offsets // 2
     blocks, piece, fields = windows[0].shape[1:]
     depth = piece * PARTS
@@ -39,7 +43,16 @@
     way = 1 - 2 * y
     z = here // 4
     at_chain = jnp.where(y == 0, z, places - 1 - z)
+    first = at_chain == 0
+    last = at_chain == places - 1
     feeds_near = x == y
+    feeds_far = x != y
+    start = jnp.logical_and(y == 0, first)
+    before_end = jnp.logical_and(y == 0, last)
+    end = jnp.logical_and(y == 1, first)
+    waits_long = jnp.logical_and(y == 1, last)
+    near_end = jnp.logical_and(feeds_near, last)
+    skips_z = jnp.logical_and(before_end, feeds_far)
 
     def panel(steps):
         return lax.rem(here + steps + panels, panels)
@@ -48,6 +61,8 @@
     to_y = panel(2 * way)
     to_z = panel(4 * way)
     from_z = panel(-4 * way)
+    to_start = panel(2)
+    to_opening = panel(3)
 
     def rows_of(part):
         return pl.ds(part * piece, piece)
@@ -62,9 +77,7 @@
         copy.start()
     scalar_copies = [
         pltpu.make_async_copy(source, target, scalar_sem.at[i])
-        for i, (source, target) in enumerate(
-            [(pairs_hbm, pairs_ref), (send_hbm, send_ref)]
-        )
+        for i, (source, target) in enumerate([(pairs_hbm, pairs_ref), (send_hbm, send_ref)])
     ]
     for copy in scalar_copies:
         copy.start()
@@ -72,6 +85,8 @@
         pltpu.make_async_copy(weights_ref.at[0, 0, k], weights.at[k], weight_sem.at[k])
         for k in range(count)
     ]
+    near_copy = pltpu.make_async_copy(near_ref, near, near_sem)
+    incident_copy = pltpu.make_async_copy(incident_ref, incident, incident_sem)
 
     barrier = pltpu.get_barrier_semaphore()
 
@@ -83,14 +98,23 @@
     greet(barrier, panel=to_x)
     greet(barrier, panel=to_y)
 
-    @pl.when(at_chain > 0)
+    @pl.when(jnp.logical_not(end))
     def _():
         greet(barrier, panel=from_z)
+
+    @pl.when(start)
+    def _():
+        greet(barrier, panel=panel(-2))
+
+        @pl.when(feeds_near)
+        def _():
+            greet(barrier, panel=panel(-3))
 
     for ahead in range(1, lags):
         greet(barrier, lag=lax.rem(lag + ahead, lags))
     pl.semaphore_wait(
-        barrier, 2 + lags - 1 + jnp.where(at_chain < places - 1, 1, 0).astype(jnp.int32)
+        barrier,
+        2 + lags - 1 + jnp.where(waits_long, 0, jnp.where(jnp.logical_or(end, skips_z), 2, 1)).astype(jnp.int32),
     )
     for copy in locals_here:
         copy.wait()
@@ -125,125 +149,219 @@
     def fourth_by_z(part, block):
         return copy_of(TRANSIT, FOURTH, 5, part, block, to_z)
 
+    def by_ring(part, block):
+        return copy_of(OWN, BEYOND, 6, part, block, to_start)
+
+    def fourth_by_ring(part, block):
+        return copy_of(ACROSS, FOURTH, 7, part, block, to_start)
+
+    def fourth_at_once(part, block):
+        return copy_of(BESIDE, FOURTH, 8, part, block, to_opening)
+
     def landing(slot, part, block):
         return copy_of(slot, slot, 0, part, block, to_x)
 
     pieces = [(part, block) for part in range(PARTS) for block in range(blocks)]
     backward = pieces[::-1]
+
     for one, other in zip(backward, pieces):
+        by_y(*other).start()
         by_x(*one).start()
-        by_y(*other).start()
-
-    @pl.when(at_chain > 0)
-    def _():
-        pl.semaphore_wait(chain_sem, 1)
-
-    @pl.when(at_chain < places - 1)
-    def _():
-        greet(chain_sem, panel=to_z)
-
-    near_copy = pltpu.make_async_copy(near_ref, near, near_sem)
-    incident_copy = pltpu.make_async_copy(incident_ref, incident, incident_sem)
+        if other[0] < RING_OWN:
+            @pl.when(jnp.logical_and(end, feeds_near))
+            def _():
+                by_ring(*other).start()
+
     for copy in weight_copies:
         copy.start()
     incident_copy.start()
     near_copy.start()
 
-    behind = 3
-    total_steps = len(pieces) + behind
-    for step in range(total_steps):
+    def pass_greeting():
+        @pl.when(jnp.logical_not(first))
+        def _():
+            pl.semaphore_wait(chain_sem, 1)
+
+        @pl.when(jnp.logical_not(last))
+        def _():
+            greet(chain_sem, panel=to_z)
+
+    @pl.when(jnp.logical_and(y == 1, at_chain <= 1))
+    def _():
+        pass_greeting()
+
+    for copy in scalar_copies:
+        copy.wait()
+    live = counts_ref[0, 0]
+    readers = partial_value.shape[0]
+    steps_of = (0, 1 - 2 * x, 2 * way, -2 * way, 2 * x - 1)
+    chosen = []
+    for steps in steps_of:
+        row = []
+        for slot in range(slots):
+            index, found, reader = 0, 0, 0
+            for k in range(count):
+                hit = jnp.logical_and(
+                    jnp.logical_and(
+                        pairs_ref[0, 0, 0, k] == reach + steps, pairs_ref[0, 1, 0, k] == slot
+                    ),
+                    k < live,
+                )
+                index = jnp.where(hit, k, index)
+                found = jnp.where(hit, 1, found)
+                reader = jnp.where(hit, pairs_ref[0, 2, 0, k], reader)
+            block = send_ref[0, reach + steps, slot, panel(steps)]
+            row.append((index, found, reader, block))
+        chosen.append(row)
+    for copy in weight_copies:
+        copy.wait()
+
+    def product(terms, at):
+        left, right = [], []
+        for place, part in terms:
+            for index, found, reader, block in chosen[place]:
+                left.append(weights[index, at, part * piece:(part + 1) * piece])
+                value = windows[part][place, 0]
+                for b in range(1, blocks):
+                    value = jnp.where(block == b, windows[part][place, b], value)
+                right.append(
+                    jnp.concatenate(
+                        [
+                            jnp.where(
+                                jnp.logical_and(found == 1, reader == r),
+                                value, jnp.zeros_like(value),
+                            )
+                            for r in range(readers)
+                        ],
+                        axis=1,
+                    )
+                )
+        return jnp.dot(
+            jnp.concatenate(left, axis=1), jnp.concatenate(right, axis=0),
+            preferred_element_type=jnp.float32,
+        )
+
+    rows = depth // CHUNKS
+    chunks = [slice(chunk * rows, (chunk + 1) * rows) for chunk in range(CHUNKS)]
+
+    def add(*terms, fresh=False):
+        for at in chunks:
+            term = product(terms, at)
+            running[at, :] = term if fresh else running[at, :] + term
+
+    add(*[(OWN, part) for part in range(PARTS)], fresh=True)
+
+    for step in range(len(pieces) + max(ASIDE, BEHIND)):
         if step < len(pieces):
-            part, block = backward[step]
-            landing(ACROSS, part, block).wait_recv()
-            if part >= max(NEAR_BY_X, FAR_BY_X):
-                fourth_by_y(part, block).start()
-            elif part >= NEAR_BY_X:
-                @pl.when(feeds_near)
+            part, block = pieces[step]
+
+            @pl.when(end)
+            def _():
+                landing(ACROSS, *backward[step]).wait_recv()
+                if backward[step][0] >= DIRECT:
+                    @pl.when(feeds_far)
+                    def _():
+                        fourth_by_ring(*backward[step]).start()
+
+            landing(BESIDE, part, block).wait_recv()
+            if part < DIRECT:
+                @pl.when(skips_z)
                 def _():
-                    fourth_by_y(part, block).start()
-            elif part >= FAR_BY_X:
-                @pl.when(jnp.logical_not(feeds_near))
+                    fourth_at_once(part, block).start()
+
+            if step < LATE_GREETING:
+                @pl.when(
+                    jnp.logical_not(
+                        jnp.logical_or(waits_long, skips_z) if part < RING_OWN else waits_long
+                    )
+                )
                 def _():
-                    fourth_by_y(part, block).start()
-            part, block = pieces[step]
-            landing(BESIDE, part, block).wait_recv()
-            by_z(part, block).start()
-            if part < NEAR_BY_X:
-                @pl.when(feeds_near)
+                    by_z(part, block).start()
+            else:
+                if step == LATE_GREETING:
+                    @pl.when(waits_long)
+                    def _():
+                        pass_greeting()
+                        for missed in pieces[:step]:
+                            by_z(*missed).start()
+
+                @pl.when(jnp.logical_not(skips_z) if part < RING_OWN else here >= 0)
                 def _():
-                    fourth_by_x(part, block).start()
-        if step >= behind:
-            part, block = pieces[step - behind]
-
-            @pl.when(jnp.logical_not(feeds_near))
+                    by_z(part, block).start()
+
+            @pl.when(feeds_near if part < NEAR_BY_X else near_end)
+            def _():
+                fourth_by_x(part, block).start()
+
+        if ASIDE <= step < len(pieces) + ASIDE:
+            turn = step - ASIDE
+            part, block = backward[turn]
+
+            @pl.when(jnp.logical_not(end))
+            def _():
+                landing(ACROSS, part, block).wait_recv()
+                if part >= NEAR_BY_X:
+                    @pl.when(jnp.logical_and(feeds_near, jnp.logical_not(first)))
+                    def _():
+                        fourth_by_y(part, block).start()
+
+                if part >= FAR_BY_X:
+                    @pl.when(feeds_far)
+                    def _():
+                        fourth_by_y(part, block).start()
+
+            if turn % blocks == blocks - 1:
+                add((BESIDE, turn // blocks))
+        if step == 1:
+            @pl.when(jnp.logical_and(y == 1, jnp.logical_and(at_chain > 1, jnp.logical_not(last))))
+            def _():
+                pass_greeting()
+        if BEHIND <= step < len(pieces) + BEHIND:
+            part, block = pieces[step - BEHIND]
+
+            @pl.when(jnp.logical_and(feeds_far, jnp.logical_not(first)))
             def _():
                 landing(BEYOND, part, block).wait_recv()
                 if part < FAR_BY_X:
                     fourth_by_x(part, block).start()
 
-    @pl.when(feeds_near)
+    @pl.when(jnp.logical_and(feeds_near, jnp.logical_not(before_end)))
     def _():
         for part, block in backward:
             if part >= FAR_BY_X:
                 landing(TRANSIT, part, block).wait_recv()
                 fourth_by_z(part, block).start()
-        for part, block in pieces:
-            landing(BEYOND, part, block).wait_recv()
-
-    for copy in scalar_copies + weight_copies:
-        copy.wait()
+
+    def arrive(place, part):
+        if place == BEYOND:
+            @pl.when(jnp.logical_or(feeds_near, first))
+            def _():
+                for block in range(blocks):
+                    landing(place, part, block).wait_recv()
+
+            if part < FAR_BY_X:
+                @pl.when(jnp.logical_and(end, feeds_far))
+                def _():
+                    for block in range(blocks):
+                        fourth_by_x(part, block).start()
+        else:
+            for block in range(blocks):
+                landing(place, part, block).wait_recv()
+
+    add(*[(ACROSS, part) for part in range(PARTS)])
+    order = [(BEYOND, 0)]
+    for part in range(1, PARTS):
+        order += [(BEYOND, part), (FOURTH, part - 1)]
+    order.append((FOURTH, PARTS - 1))
+    for place, part in order[:-1]:
+        arrive(place, part)
+        add((place, part))
     incident_copy.wait()
     near_copy.wait()
-
-    live = counts_ref[0, 0]
-    readers = right.shape[2] // fields
-    chosen = []
-    for k in range(count):
-        offset = pairs_ref[0, 0, 0, k]
-        slot = pairs_ref[0, 1, 0, k]
-        reader = pairs_ref[0, 2, 0, k]
-        steps = offset - reach
-        block = send_ref[0, offset, slot, panel(steps)]
-        place = jnp.where(
-            steps == 0, OWN,
-            jnp.where(
-                steps == 1 - 2 * x, ACROSS,
-                jnp.where(
-                    steps == 2 * way, BESIDE, jnp.where(steps == -2 * way, BEYOND, FOURTH)
-                ),
-            ),
-        )
-        chosen.append((place, block, reader))
-
-    def arrive(part):
-        for block in range(blocks):
-            landing(FOURTH, part, block).wait_recv()
-        for k, (place, block, reader) in enumerate(chosen):
-            value = windows[part][place, block]
-            for r in range(readers):
-                kept = jnp.logical_and(reader == r, k < live)
-                right[part, k * piece:(k + 1) * piece, r * fields:(r + 1) * fields] = jnp.where(
-                    kept, value, jnp.zeros_like(value)
-                )
-
-    def product(part, at):
-        left = jnp.concatenate(
-            [weights[k, at, part * piece:(part + 1) * piece] for k in range(count)], axis=1
-        )
-        return jnp.dot(left, right[part], preferred_element_type=jnp.float32)
-
-    rows = depth // CHUNKS
+    arrive(*order[-1])
     sums = []
-    for part in ORDER[:-1]:
-        arrive(part)
-        for chunk in range(CHUNKS):
-            at = slice(chunk * rows, (chunk + 1) * rows)
-            term = product(part, at)
-            running[at, :] = term if part == ORDER[0] else running[at, :] + term
-    arrive(ORDER[-1])
-    for chunk in range(CHUNKS):
-        at = slice(chunk * rows, (chunk + 1) * rows)
-        total = running[at, :] + product(ORDER[-1], at)
+    for chunk, at in enumerate(chunks):
+        total = running[at, :] + product(order[-1:], at)
         for r in range(readers):
             partial_value[r, at, :] = total[:, r * fields:(r + 1) * fields]
         for ahead in range(1, lags):
@@ -258,39 +376,64 @@
             )
             copy.start()
             sums.append(copy)
+    far_inner = jnp.logical_and(feeds_far, jnp.logical_not(first))
     for part, block in pieces:
         by_x(part, block).wait_send()
         by_y(part, block).wait_send()
-        by_z(part, block).wait_send()
-
-    @pl.when(feeds_near)
-    def _():
-        for part, block in pieces:
-            if part < NEAR_BY_X:
-                fourth_by_x(part, block).wait_send()
-            else:
+
+        @pl.when(jnp.logical_not(skips_z) if part < RING_OWN else here >= 0)
+        def _():
+            by_z(part, block).wait_send()
+
+        near_x = feeds_near if part < NEAR_BY_X else near_end
+        end_far = jnp.logical_and(end, feeds_far)
+        far_x = jnp.logical_and(jnp.logical_or(far_inner, end_far), part < FAR_BY_X)
+
+        @pl.when(jnp.logical_or(near_x, far_x))
+        def _():
+            fourth_by_x(part, block).wait_send()
+
+        if part >= NEAR_BY_X:
+            @pl.when(jnp.logical_and(feeds_near, jnp.logical_not(first)))
+            def _():
                 fourth_by_y(part, block).wait_send()
-            if part >= FAR_BY_X:
+
+        if part >= FAR_BY_X:
+            @pl.when(jnp.logical_and(feeds_far, jnp.logical_not(end)))
+            def _():
+                fourth_by_y(part, block).wait_send()
+
+            @pl.when(jnp.logical_and(feeds_near, jnp.logical_not(before_end)))
+            def _():
                 fourth_by_z(part, block).wait_send()
 
-    @pl.when(jnp.logical_not(feeds_near))
-    def _():
-        for part, block in pieces:
-            if part < FAR_BY_X:
-                fourth_by_x(part, block).wait_send()
-            else:
-                fourth_by_y(part, block).wait_send()
-
-    for copy in sums:
-        copy.wait_recv()
+        if part < RING_OWN:
+            @pl.when(jnp.logical_and(end, feeds_near))
+            def _():
+                by_ring(part, block).wait_send()
+
+        if part < DIRECT:
+            @pl.when(skips_z)
+            def _():
+                fourth_at_once(part, block).wait_send()
+        else:
+            @pl.when(end_far)
+            def _():
+                fourth_by_ring(part, block).wait_send()
+
+    solved = [None] * own
+    for chunk, at in enumerate(chunks):
+        for copy in sums[chunk * (lags - 1):(chunk + 1) * (lags - 1)]:
+            copy.wait_recv()
+        for j in range(own):
+            summed = partial_value[lag * own + j, at]
+            for ahead in range(1, lags):
+                summed = summed + landed[ahead - 1, j, at]
+            remainder = (incident[j, at].astype(jnp.float32) - summed).astype(jnp.bfloat16)
+            term = jnp.dot(near[j, :, at], remainder, preferred_element_type=jnp.float32)
+            solved[j] = term if chunk == 0 else solved[j] + term
     for j in range(own):
-        summed = partial_value[lag * own + j]
-        for ahead in range(1, lags):
-            summed = summed + landed[ahead - 1, j]
-        remainder = (incident[j].astype(jnp.float32) - summed).astype(jnp.bfloat16)
-        out_ref[j] = jnp.dot(
-            near[j], remainder, preferred_element_type=jnp.float32
-        ).astype(out_ref.dtype)
+        out_ref[j] = solved[j].astype(out_ref.dtype)
     for copy in sums:
         copy.wait_send()
 
@@ -321,11 +464,10 @@
             pltpu.VMEM(weights.shape[2:], weights.dtype),
             pltpu.VMEM(near_inverse.shape, near_inverse.dtype),
             pltpu.VMEM(incident.shape, incident.dtype),
-            pltpu.VMEM((PARTS, count * piece, readers * fields), history.dtype),
             pltpu.VMEM((depth, readers * fields), jnp.float32),
             pltpu.VMEM((readers, depth, fields), jnp.float32),
             pltpu.VMEM((lags - 1, own, depth, fields), jnp.float32),
-            dma((6, PARTS, readers)),
+            dma((9, PARTS, readers)),
             dma((TRANSIT, PARTS, readers)),
             dma((PARTS,)),
             dma((count,)),

time: 22.9 us -> 21.5 us (0.939)
  Pallas kernels: 21.4 us -> 20.1 us
    pallas_call x1, Pallas kernels: 21.4 us -> 20.1 us  [relayed(): pl.pallas_call(functools.partial(relay_kernel, panels, lags), out_shape=p...]
where the time goes in v2:
time: 21.5 us; the launch traced here: 21.4 us
  Pallas kernels  20.1 us (93%)
  local copies, waits for them, and re-layouts  0.66 us (3%)
  between operations  0.66 us (3%)
    pallas_call x1, Pallas kernels, relayed(): pl.pallas_call(functools.partial(relay_kernel, panels, lags), out_shape=p...  20.1 us
    unnamed x1, local copies, waits for them, and re-layouts  0.66 us

profile of v2, /device:TPU:1, one launch (start us, length us, event | category | flops | bytes accessed | tf_op | source)
XLA Modules:
  0.0 21.4 jit_solution(7813385421766828989)
XLA Ops:
  0.7 20.1 %shard_map.73 = bf16[1,512,128]{2,1,0:T(8,128)(2,1)S(1)} custom-call(s32[1,1]{1,0:T(1,128)S(6)} %copy.10.counts_ref, s32[1,3,1,6]{3,2,1,0:T(1,128)} %bitcast.3, s32[1,5,2,16]{3,2,1,0:T(2,128)} %bitcast.2, bf16[1,2,512,128]{3,2,1,0:T(8,128)(2,1)} %local_ref.1, bf16[1,1,6,512,512]{4,3,2,1,0:T(8,128)(2,1)} %weights_ref.1, bf16[1,512,128]{2,1,0:T(8,128)(2,1)} %incident_ref.1, ...), custom_call_target="tpu_custom_call" | custom-call | tf_op jit(solution)/shard_map/pallas_call | solution.py:455
  20.7 0.7 %copy.9 = bf16[1,512,128]{2,1,0:T(8,128)(2,1)} copy(bf16[1,512,128]{2,1,0:T(8,128)(2,1)S(1)} %shard_map.73) | data formatting | bytes 262144

commit v3 on v2

--- a/solution.py
+++ b/solution.py
@@ -14,6 +14,7 @@
 FAR_BY_X = 3
 RING_OWN = 1
 DIRECT = 2
+STRAIGHT = (2,)
 OWN, ACROSS, BESIDE, BEYOND, FOURTH, TRANSIT = range(6)
 BEHIND = 5
 ASIDE = 3
@@ -62,14 +63,14 @@
     to_z = panel(4 * way)
     from_z = panel(-4 * way)
     to_start = panel(2)
-    to_opening = panel(3)
+    to_first = panel(3)
 
     def rows_of(part):
         return pl.ds(part * piece, piece)
 
     locals_here = [
         pltpu.make_async_copy(
-            local_ref.at[0, :, rows_of(part)], windows[part].at[OWN], local_sem.at[part]
+            local_ref.at[0, :, rows_of(part)], windows[part].at[OWN], local_sem
         )
         for part in range(PARTS)
     ]
@@ -82,8 +83,7 @@
     for copy in scalar_copies:
         copy.start()
     weight_copies = [
-        pltpu.make_async_copy(weights_ref.at[0, 0, k], weights.at[k], weight_sem.at[k])
-        for k in range(count)
+        pltpu.make_async_copy(weights_ref.at[0, 0], weights, weight_sem)
     ]
     near_copy = pltpu.make_async_copy(near_ref, near, near_sem)
     incident_copy = pltpu.make_async_copy(incident_ref, incident, incident_sem)
@@ -109,22 +109,46 @@
         @pl.when(feeds_near)
         def _():
             greet(barrier, panel=panel(-3))
+            greet(barrier, panel=panel(-1))
 
     for ahead in range(1, lags):
         greet(barrier, lag=lax.rem(lag + ahead, lags))
     pl.semaphore_wait(
         barrier,
-        2 + lags - 1 + jnp.where(waits_long, 0, jnp.where(jnp.logical_or(end, skips_z), 2, 1)).astype(jnp.int32),
+        1
+        + lags
+        + jnp.where(
+            waits_long, 0,
+            jnp.where(end, jnp.where(feeds_near, 3, 2), jnp.where(skips_z, 2, 1)),
+        ).astype(jnp.int32),
     )
-    for copy in locals_here:
-        copy.wait()
-
-    def copy_of(source, target, link, part, block, device):
+    pltpu.make_async_copy(local_ref.at[0], local_ref.at[0], local_sem).wait()
+
+    pieces = [(part, block) for part in range(PARTS) for block in range(blocks)]
+    backward = pieces[::-1]
+
+    alone = min(NEAR_BY_X, FAR_BY_X)
+    each = PARTS * blocks
+    relayed_across = (PARTS - alone) * blocks
+
+    def arrival(target, part, block):
+        if target == BESIDE:
+            return part * blocks + block
+        if target == BEYOND:
+            return each + part * blocks + block
+        if target == ACROSS:
+            place = (part - alone) * blocks + block if part >= alone else relayed_across
+            return 2 * each + place
+        if target == FOURTH:
+            return 2 * each + relayed_across + 1 + part
+        return 2 * each + relayed_across + 1 + PARTS + (part - FAR_BY_X) * blocks + block
+
+    def copy_of(source, target, link, part, block, device, lands=None):
         return pltpu.make_async_remote_copy(
             src_ref=windows[part].at[source, block],
             dst_ref=windows[part].at[target, block],
-            send_sem=send_sem.at[link, part, block],
-            recv_sem=recv_sem.at[target - 1, part, block],
+            send_sem=send_sem.at[link],
+            recv_sem=recv_sem.at[arrival(target, part, block) if lands is None else lands],
             device_id={"panel": device},
             device_id_type=pl.DeviceIdType.MESH,
         )
@@ -133,36 +157,50 @@
         return copy_of(OWN, ACROSS, 0, part, block, to_x)
 
     def by_y(part, block):
-        return copy_of(OWN, BESIDE, 1, part, block, to_y)
+        return copy_of(OWN, BESIDE, 0, part, block, to_y)
 
     def by_z(part, block):
-        return copy_of(BESIDE, BEYOND, 2, part, block, to_z)
+        return copy_of(BESIDE, BEYOND, 0, part, block, to_z)
 
     def fourth_by_x(part, block):
-        return copy_of(jnp.where(feeds_near, BESIDE, BEYOND), FOURTH, 3, part, block, to_x)
+        return copy_of(jnp.where(feeds_near, BESIDE, BEYOND), FOURTH, 1, part, block, to_x)
 
     def fourth_by_y(part, block):
+        if part < FAR_BY_X:
+            return copy_of(ACROSS, FOURTH, 1, part, block, to_y)
+        lands = jnp.where(
+            feeds_near, arrival(FOURTH, part, block), arrival(TRANSIT, part, block)
+        )
         return copy_of(
-            ACROSS, jnp.where(feeds_near, FOURTH, TRANSIT), 4, part, block, to_y
+            ACROSS, jnp.where(feeds_near, FOURTH, TRANSIT), 1, part, block, to_y, lands
         )
 
     def fourth_by_z(part, block):
-        return copy_of(TRANSIT, FOURTH, 5, part, block, to_z)
+        return copy_of(TRANSIT, FOURTH, 1, part, block, to_z)
 
     def by_ring(part, block):
-        return copy_of(OWN, BEYOND, 6, part, block, to_start)
+        return copy_of(OWN, BEYOND, 1, part, block, to_start)
 
     def fourth_by_ring(part, block):
-        return copy_of(ACROSS, FOURTH, 7, part, block, to_start)
+        return copy_of(ACROSS, FOURTH, 1, part, block, to_start)
 
     def fourth_at_once(part, block):
-        return copy_of(BESIDE, FOURTH, 8, part, block, to_opening)
+        return copy_of(BESIDE, FOURTH, 1, part, block, to_first)
+
+    def fourth_straight(part, block):
+        return copy_of(OWN, FOURTH, 1, part, block, panel(1))
 
     def landing(slot, part, block):
         return copy_of(slot, slot, 0, part, block, to_x)
 
-    pieces = [(part, block) for part in range(PARTS) for block in range(blocks)]
-    backward = pieces[::-1]
+    def bulk(number, link, lands):
+        rows = number * piece * fields // (2 * weights.shape[2])
+        stretch = weights.at[pl.ds(0, 2), pl.ds(0, rows)]
+        return pltpu.make_async_remote_copy(
+            src_ref=stretch, dst_ref=stretch,
+            send_sem=send_sem.at[link], recv_sem=recv_sem.at[lands],
+            device_id={"panel": to_x}, device_id_type=pl.DeviceIdType.MESH,
+        )
 
     for one, other in zip(backward, pieces):
         by_y(*other).start()
@@ -171,6 +209,11 @@
             @pl.when(jnp.logical_and(end, feeds_near))
             def _():
                 by_ring(*other).start()
+
+        if other[0] in STRAIGHT:
+            @pl.when(jnp.logical_and(end, feeds_near))
+            def _():
+                fourth_straight(*other).start()
 
     for copy in weight_copies:
         copy.start()
@@ -257,8 +300,9 @@
 
             @pl.when(end)
             def _():
-                landing(ACROSS, *backward[step]).wait_recv()
-                if backward[step][0] >= DIRECT:
+                if backward[step][0] >= alone:
+                    landing(ACROSS, *backward[step]).wait_recv()
+                if backward[step][0] >= DIRECT and backward[step][0] not in STRAIGHT:
                     @pl.when(feeds_far)
                     def _():
                         fourth_by_ring(*backward[step]).start()
@@ -299,7 +343,8 @@
 
             @pl.when(jnp.logical_not(end))
             def _():
-                landing(ACROSS, part, block).wait_recv()
+                if part >= alone:
+                    landing(ACROSS, part, block).wait_recv()
                 if part >= NEAR_BY_X:
                     @pl.when(jnp.logical_and(feeds_near, jnp.logical_not(first)))
                     def _():
@@ -345,9 +390,9 @@
                     for block in range(blocks):
                         fourth_by_x(part, block).start()
         else:
-            for block in range(blocks):
-                landing(place, part, block).wait_recv()
-
+            bulk(blocks, 0, arrival(FOURTH, part, 0)).wait_recv()
+
+    bulk(alone * blocks, 0, arrival(ACROSS, 0, 0)).wait_recv()
     add(*[(ACROSS, part) for part in range(PARTS)])
     order = [(BEYOND, 0)]
     for part in range(1, PARTS):
@@ -369,57 +414,47 @@
             copy = pltpu.make_async_remote_copy(
                 src_ref=partial_value.at[pl.ds(other * own, own), pl.ds(chunk * rows, rows)],
                 dst_ref=landed.at[ahead - 1, :, pl.ds(chunk * rows, rows)],
-                send_sem=sum_send_sem.at[ahead - 1, chunk],
+                send_sem=sum_send_sem.at[ahead - 1],
                 recv_sem=sum_recv_sem.at[ahead - 1, chunk],
                 device_id={"lag": other},
                 device_id_type=pl.DeviceIdType.MESH,
             )
             copy.start()
             sums.append(copy)
-    far_inner = jnp.logical_and(feeds_far, jnp.logical_not(first))
-    for part, block in pieces:
-        by_x(part, block).wait_send()
-        by_y(part, block).wait_send()
-
-        @pl.when(jnp.logical_not(skips_z) if part < RING_OWN else here >= 0)
+    def parts_of(taken):
+        return blocks * len([part for part in range(PARTS) if taken(part)])
+
+    def when(condition, number):
+        return jnp.where(condition, number, 0).astype(jnp.int32)
+
+    near_x, far_x = NEAR_BY_X * blocks, FAR_BY_X * blocks
+    ringed, at_once = RING_OWN * blocks, DIRECT * blocks
+    straight = parts_of(lambda part: part in STRAIGHT)
+    extra = jnp.where(
+        feeds_near,
+        near_x
+        + when(near_end, each - near_x)
+        + when(jnp.logical_not(first), each - near_x)
+        + when(jnp.logical_not(before_end), each - far_x)
+        + when(end, ringed + straight),
+        when(jnp.logical_not(first), far_x)
+        + when(jnp.logical_not(end), each - far_x)
+        + when(end, far_x + each - straight - at_once)
+        + when(before_end, at_once),
+    )
+
+    @pl.when(skips_z)
+    def _():
+        bulk(3 * each - ringed, 0, 0).wait_send()
+
+    @pl.when(jnp.logical_not(skips_z))
+    def _():
+        bulk(3 * each, 0, 0).wait_send()
+
+    for number in range(blocks, 3 * each, blocks):
+        @pl.when(extra == number)
         def _():
-            by_z(part, block).wait_send()
-
-        near_x = feeds_near if part < NEAR_BY_X else near_end
-        end_far = jnp.logical_and(end, feeds_far)
-        far_x = jnp.logical_and(jnp.logical_or(far_inner, end_far), part < FAR_BY_X)
-
-        @pl.when(jnp.logical_or(near_x, far_x))
-        def _():
-            fourth_by_x(part, block).wait_send()
-
-        if part >= NEAR_BY_X:
-            @pl.when(jnp.logical_and(feeds_near, jnp.logical_not(first)))
-            def _():
-                fourth_by_y(part, block).wait_send()
-
-        if part >= FAR_BY_X:
-            @pl.when(jnp.logical_and(feeds_far, jnp.logical_not(end)))
-            def _():
-                fourth_by_y(part, block).wait_send()
-
-            @pl.when(jnp.logical_and(feeds_near, jnp.logical_not(before_end)))
-            def _():
-                fourth_by_z(part, block).wait_send()
-
-        if part < RING_OWN:
-            @pl.when(jnp.logical_and(end, feeds_near))
-            def _():
-                by_ring(part, block).wait_send()
-
-        if part < DIRECT:
-            @pl.when(skips_z)
-            def _():
-                fourth_at_once(part, block).wait_send()
-        else:
-            @pl.when(end_far)
-            def _():
-                fourth_by_ring(part, block).wait_send()
+            bulk(number, 1, 0).wait_send()
 
     solved = [None] * own
     for chunk, at in enumerate(chunks):
@@ -434,8 +469,14 @@
             solved[j] = term if chunk == 0 else solved[j] + term
     for j in range(own):
         out_ref[j] = solved[j].astype(out_ref.dtype)
-    for copy in sums:
-        copy.wait_send()
+    for ahead in range(1, lags):
+        whole = partial_value.at[pl.ds(0, own)]
+        pltpu.make_async_remote_copy(
+            src_ref=whole, dst_ref=whole,
+            send_sem=sum_send_sem.at[ahead - 1], recv_sem=sum_recv_sem.at[ahead - 1, 0],
+            device_id={"lag": lax.rem(lag + ahead, lags)},
+            device_id_type=pl.DeviceIdType.MESH,
+        ).wait_send()
 
 
 def relayed(panels, lags, history, weights, pairs, counts, send_list, incident, near_inverse):
@@ -443,6 +484,9 @@
     count = weights.shape[2]
     own = incident.shape[0]
     piece = depth // PARTS
+    arrivals = PARTS * (2 * readers + 1) + 1 + readers * (
+        2 * PARTS - min(NEAR_BY_X, FAR_BY_X) - FAR_BY_X
+    )
     in_hbm = pl.BlockSpec(memory_space=pltpu.HBM)
     dma = pltpu.SemaphoreType.DMA
     held = [
@@ -467,13 +511,13 @@
             pltpu.VMEM((depth, readers * fields), jnp.float32),
             pltpu.VMEM((readers, depth, fields), jnp.float32),
             pltpu.VMEM((lags - 1, own, depth, fields), jnp.float32),
-            dma((9, PARTS, readers)),
-            dma((TRANSIT, PARTS, readers)),
-            dma((PARTS,)),
-            dma((count,)),
+            dma((2,)),
+            dma((arrivals,)),
             dma,
             dma,
-            dma((lags - 1, CHUNKS)),
+            dma,
+            dma,
+            dma((lags - 1,)),
             dma((lags - 1, CHUNKS)),
             pltpu.SemaphoreType.REGULAR,
         ],

time: 21.5 us -> 19.8 us (0.921)
  Pallas kernels: 20.1 us -> 18.4 us
    pallas_call x1, Pallas kernels: 20.1 us -> 18.4 us  [relayed(): pl.pallas_call(functools.partial(relay_kernel, panels, lags), out_shape=p...]
where the time goes in v3:
time: 19.8 us; the launch traced here: 19.7 us
  Pallas kernels  18.4 us (93%)
  local copies, waits for them, and re-layouts  0.66 us (3%)
  between operations  0.66 us (3%)
    pallas_call x1, Pallas kernels, relayed(): pl.pallas_call(functools.partial(relay_kernel, panels, lags), out_shape=p...  18.4 us
    unnamed x1, local copies, waits for them, and re-layouts  0.66 us

profile of v3, /device:TPU:1, one launch (start us, length us, event | category | flops | bytes accessed | tf_op | source)
XLA Modules:
  0.0 19.7 jit_solution(9303217211873146217)
XLA Ops:
  0.7 18.4 %shard_map.73 = bf16[1,512,128]{2,1,0:T(8,128)(2,1)S(1)} custom-call(s32[1,1]{1,0:T(1,128)S(6)} %copy.10.counts_ref, s32[1,3,1,6]{3,2,1,0:T(1,128)} %bitcast.3, s32[1,5,2,16]{3,2,1,0:T(2,128)} %bitcast.2, bf16[1,2,512,128]{3,2,1,0:T(8,128)(2,1)} %local_ref.1, bf16[1,1,6,512,512]{4,3,2,1,0:T(8,128)(2,1)} %weights_ref.1, bf16[1,512,128]{2,1,0:T(8,128)(2,1)} %incident_ref.1, ...), custom_call_target="tpu_custom_call" | custom-call | tf_op jit(solution)/shard_map/pallas_call | solution.py:499
  19.0 0.7 %copy.9 = bf16[1,512,128]{2,1,0:T(8,128)(2,1)} copy(bf16[1,512,128]{2,1,0:T(8,128)(2,1)S(1)} %shard_map.73) | data formatting | bytes 262144

commit v4 on v3

--- a/solution.py
+++ b/solution.py
@@ -12,10 +12,15 @@
 
 NEAR_BY_X = 2
 FAR_BY_X = 3
-RING_OWN = 1
-DIRECT = 2
-STRAIGHT = (2,)
-OWN, ACROSS, BESIDE, BEYOND, FOURTH, TRANSIT = range(6)
+RING = (2,)
+RING_FAR = ()
+AT_ONCE = (0,)
+STRAIGHT = (1,)
+HANDED = (3,)
+RING_STEP = 5
+DEFERRED = 2
+SPLIT = 1
+OWN, ACROSS, BESIDE, BEYOND, FOURTH, TRANSIT, LASTING = range(7)
 BEHIND = 5
 ASIDE = 3
 LATE_GREETING = 3
@@ -26,7 +31,7 @@
     counts_ref, pairs_hbm, send_hbm, local_ref, weights_ref, incident_ref, near_ref,
     out_ref,
     pairs_ref, send_ref, scalar_sem,
-    windows, weights, near, incident, running, partial_value, landed,
+    windows, weights, near, incident, running, theirs, mine, landed,
     send_sem, recv_sem, local_sem, weight_sem, near_sem, incident_sem,
     sum_send_sem, sum_recv_sem, chain_sem,
 ):
@@ -34,7 +39,9 @@
     lag = lax.axis_index("lag")
     offsets, slots = send_ref.shape[1:3]
     reach = offsets // 2
-    blocks, piece, fields = windows[0].shape[1:]
+    subs, small, fields = windows[0].shape[1:]
+    blocks = subs // SPLIT
+    piece = small * SPLIT
     depth = piece * PARTS
     count = weights.shape[0]
     own = incident.shape[0]
@@ -52,8 +59,22 @@
     before_end = jnp.logical_and(y == 0, last)
     end = jnp.logical_and(y == 1, first)
     waits_long = jnp.logical_and(y == 1, last)
-    near_end = jnp.logical_and(feeds_near, last)
+    near_end = jnp.logical_and(feeds_near, jnp.logical_or(before_end, start))
+    near_aside = jnp.logical_and(
+        feeds_near, jnp.logical_not(jnp.logical_or(end, waits_long))
+    )
     skips_z = jnp.logical_and(before_end, feeds_far)
+    skips_far = jnp.logical_and(before_end, feeds_near)
+    start_far = jnp.logical_and(start, feeds_far)
+
+    def stays(part, block):
+        skipped = here < 0
+        if part in RING or (part, block) in deferred:
+            skipped = jnp.logical_or(skipped, skips_z)
+        if part in RING_FAR:
+            skipped = jnp.logical_or(skipped, skips_far)
+        return skipped
+
 
     def panel(steps):
         return lax.rem(here + steps + panels, panels)
@@ -65,14 +86,14 @@
     to_start = panel(2)
     to_first = panel(3)
 
-    def rows_of(part):
-        return pl.ds(part * piece, piece)
-
     locals_here = [
         pltpu.make_async_copy(
-            local_ref.at[0, :, rows_of(part)], windows[part].at[OWN], local_sem
+            local_ref.at[0, sub // SPLIT, pl.ds(part * piece + sub % SPLIT * small, small)],
+            windows[part].at[OWN, sub],
+            local_sem,
         )
         for part in range(PARTS)
+        for sub in range(subs)
     ]
     for copy in locals_here:
         copy.start()
@@ -124,24 +145,24 @@
     )
     pltpu.make_async_copy(local_ref.at[0], local_ref.at[0], local_sem).wait()
 
-    pieces = [(part, block) for part in range(PARTS) for block in range(blocks)]
+    pieces = [(part, sub) for part in range(PARTS) for sub in range(subs)]
     backward = pieces[::-1]
 
     alone = min(NEAR_BY_X, FAR_BY_X)
-    each = PARTS * blocks
-    relayed_across = (PARTS - alone) * blocks
+    each = PARTS * subs
+    relayed_across = (PARTS - alone) * subs
 
     def arrival(target, part, block):
         if target == BESIDE:
-            return part * blocks + block
+            return part * subs + block
         if target == BEYOND:
-            return each + part * blocks + block
+            return each + part * subs + block
         if target == ACROSS:
-            place = (part - alone) * blocks + block if part >= alone else relayed_across
+            place = (part - alone) * subs + block if part >= alone else relayed_across
             return 2 * each + place
         if target == FOURTH:
             return 2 * each + relayed_across + 1 + part
-        return 2 * each + relayed_across + 1 + PARTS + (part - FAR_BY_X) * blocks + block
+        return 2 * each + relayed_across + 1 + PARTS + (part - FAR_BY_X) * subs + block
 
     def copy_of(source, target, link, part, block, device, lands=None):
         return pltpu.make_async_remote_copy(
@@ -194,7 +215,7 @@
         return copy_of(slot, slot, 0, part, block, to_x)
 
     def bulk(number, link, lands):
-        rows = number * piece * fields // (2 * weights.shape[2])
+        rows = number * small * fields // (2 * weights.shape[2])
         stretch = weights.at[pl.ds(0, 2), pl.ds(0, rows)]
         return pltpu.make_async_remote_copy(
             src_ref=stretch, dst_ref=stretch,
@@ -205,8 +226,13 @@
     for one, other in zip(backward, pieces):
         by_y(*other).start()
         by_x(*one).start()
-        if other[0] < RING_OWN:
+        if other[0] in RING:
             @pl.when(jnp.logical_and(end, feeds_near))
+            def _():
+                by_ring(*other).start()
+
+        if other[0] in RING_FAR:
+            @pl.when(jnp.logical_and(end, feeds_far))
             def _():
                 by_ring(*other).start()
 
@@ -236,7 +262,7 @@
     for copy in scalar_copies:
         copy.wait()
     live = counts_ref[0, 0]
-    readers = partial_value.shape[0]
+    readers = running.shape[0]
     steps_of = (0, 1 - 2 * x, 2 * way, -2 * way, 2 * x - 1)
     chosen = []
     for steps in steps_of:
@@ -259,26 +285,34 @@
     for copy in weight_copies:
         copy.wait()
 
-    def product(terms, at):
+    z_last = jnp.logical_and(start, feeds_near)
+    lasting_place = (jnp.where(z_last, FOURTH, BEYOND), jnp.where(z_last, BEYOND, FOURTH))
+    pairs_of = list(zip(chosen[FOURTH], chosen[BEYOND]))
+    lasting = (
+        [[jnp.where(z_last, f, b) for f, b in zip(*both)] for both in pairs_of],
+        [[jnp.where(z_last, b, f) for f, b in zip(*both)] for both in pairs_of],
+    )
+
+    def block_of(part, place, b):
+        return windows[part][place, b * SPLIT:(b + 1) * SPLIT].reshape((piece, fields))
+
+    def product(terms, at, columns):
         left, right = [], []
         for place, part in terms:
-            for index, found, reader, block in chosen[place]:
+            entries = chosen[place] if place < LASTING else lasting[place - LASTING]
+            place = place if place < LASTING else lasting_place[place - LASTING]
+            for index, found, reader, block in entries:
                 left.append(weights[index, at, part * piece:(part + 1) * piece])
-                value = windows[part][place, 0]
+                value = block_of(part, place, 0)
                 for b in range(1, blocks):
-                    value = jnp.where(block == b, windows[part][place, b], value)
-                right.append(
-                    jnp.concatenate(
-                        [
-                            jnp.where(
-                                jnp.logical_and(found == 1, reader == r),
-                                value, jnp.zeros_like(value),
-                            )
-                            for r in range(readers)
-                        ],
-                        axis=1,
+                    value = jnp.where(block == b, block_of(part, place, b), value)
+                kept = [
+                    jnp.where(
+                        jnp.logical_and(found == 1, reader == r), value, jnp.zeros_like(value)
                     )
-                )
+                    for r in columns
+                ]
+                right.append(jnp.concatenate(kept, axis=1))
         return jnp.dot(
             jnp.concatenate(left, axis=1), jnp.concatenate(right, axis=0),
             preferred_element_type=jnp.float32,
@@ -289,10 +323,14 @@
 
     def add(*terms, fresh=False):
         for at in chunks:
-            term = product(terms, at)
-            running[at, :] = term if fresh else running[at, :] + term
+            term = product(terms, at, range(readers))
+            for r in range(readers):
+                column = term[:, r * fields:(r + 1) * fields]
+                running[r, at] = column if fresh else running[r, at] + column
 
     add(*[(OWN, part) for part in range(PARTS)], fresh=True)
+
+    deferred = [(part, block) for part, block in pieces if part in AT_ONCE][:DEFERRED]
 
     for step in range(len(pieces) + max(ASIDE, BEHIND)):
         if step < len(pieces):
@@ -302,23 +340,19 @@
             def _():
                 if backward[step][0] >= alone:
                     landing(ACROSS, *backward[step]).wait_recv()
-                if backward[step][0] >= DIRECT and backward[step][0] not in STRAIGHT:
+                if backward[step][0] in HANDED:
                     @pl.when(feeds_far)
                     def _():
                         fourth_by_ring(*backward[step]).start()
 
             landing(BESIDE, part, block).wait_recv()
-            if part < DIRECT:
+            if part in AT_ONCE:
                 @pl.when(skips_z)
                 def _():
                     fourth_at_once(part, block).start()
 
             if step < LATE_GREETING:
-                @pl.when(
-                    jnp.logical_not(
-                        jnp.logical_or(waits_long, skips_z) if part < RING_OWN else waits_long
-                    )
-                )
+                @pl.when(jnp.logical_not(jnp.logical_or(waits_long, stays(part, block))))
                 def _():
                     by_z(part, block).start()
             else:
@@ -329,9 +363,23 @@
                         for missed in pieces[:step]:
                             by_z(*missed).start()
 
-                @pl.when(jnp.logical_not(skips_z) if part < RING_OWN else here >= 0)
+                @pl.when(jnp.logical_not(stays(part, block)))
                 def _():
                     by_z(part, block).start()
+
+            if deferred and (part, block) == deferred[-1]:
+                @pl.when(skips_z)
+                def _():
+                    for missed in deferred:
+                        by_z(*missed).start()
+
+            if step == RING_STEP:
+                @pl.when(start_far)
+                def _():
+                    for ring_part, ring_block in pieces:
+                        if ring_part in RING:
+                            landing(BEYOND, ring_part, ring_block).wait_recv()
+                            fourth_by_x(ring_part, ring_block).start()
 
             @pl.when(feeds_near if part < NEAR_BY_X else near_end)
             def _():
@@ -346,7 +394,7 @@
                 if part >= alone:
                     landing(ACROSS, part, block).wait_recv()
                 if part >= NEAR_BY_X:
-                    @pl.when(jnp.logical_and(feeds_near, jnp.logical_not(first)))
+                    @pl.when(near_aside)
                     def _():
                         fourth_by_y(part, block).start()
 
@@ -355,9 +403,9 @@
                     def _():
                         fourth_by_y(part, block).start()
 
-            if turn % blocks == blocks - 1:
-                add((BESIDE, turn // blocks))
-        if step == 1:
+            if turn % subs == subs - 1:
+                add((BESIDE, turn // subs))
+        if step == 2 * SPLIT - 1:
             @pl.when(jnp.logical_and(y == 1, jnp.logical_and(at_chain > 1, jnp.logical_not(last))))
             def _():
                 pass_greeting()
@@ -369,6 +417,12 @@
                 landing(BEYOND, part, block).wait_recv()
                 if part < FAR_BY_X:
                     fourth_by_x(part, block).start()
+
+        if step == len(pieces) - 1:
+            bulk(alone * subs, 0, arrival(ACROSS, 0, 0)).wait_recv()
+            add(*[(ACROSS, part) for part in range(alone)])
+        if step == len(pieces) + ASIDE - 1:
+            add(*[(ACROSS, part) for part in range(alone, PARTS)])
 
     @pl.when(jnp.logical_and(feeds_near, jnp.logical_not(before_end)))
     def _():
@@ -378,41 +432,52 @@
                 fourth_by_z(part, block).start()
 
     def arrive(place, part):
+        if place >= LASTING:
+            @pl.when(z_last if place == LASTING else jnp.logical_not(z_last))
+            def _():
+                arrive(FOURTH, part)
+
+            @pl.when(z_last if place > LASTING else jnp.logical_not(z_last))
+            def _():
+                arrive(BEYOND, part)
+
+            return
         if place == BEYOND:
-            @pl.when(jnp.logical_or(feeds_near, first))
-            def _():
-                for block in range(blocks):
+            @pl.when(jnp.logical_or(feeds_near, end if part in RING else first))
+            def _():
+                for block in range(subs):
                     landing(place, part, block).wait_recv()
 
             if part < FAR_BY_X:
                 @pl.when(jnp.logical_and(end, feeds_far))
                 def _():
-                    for block in range(blocks):
+                    for block in range(subs):
                         fourth_by_x(part, block).start()
         else:
-            bulk(blocks, 0, arrival(FOURTH, part, 0)).wait_recv()
-
-    bulk(alone * blocks, 0, arrival(ACROSS, 0, 0)).wait_recv()
-    add(*[(ACROSS, part) for part in range(PARTS)])
-    order = [(BEYOND, 0)]
-    for part in range(1, PARTS):
-        order += [(BEYOND, part), (FOURTH, part - 1)]
-    order.append((FOURTH, PARTS - 1))
-    for place, part in order[:-1]:
-        arrive(place, part)
-        add((place, part))
+            bulk(subs, 0, arrival(FOURTH, part, 0)).wait_recv()
+
+    order = [((BEYOND, 0), (BEYOND, 1))]
+    order += [((FOURTH, part - 2), (BEYOND, part)) for part in range(2, PARTS - 1)]
+    order += [((FOURTH, part),) for part in range(PARTS - 3, PARTS - 2)]
+    order += [((FOURTH, PARTS - 2), (LASTING, PARTS - 1)), ((LASTING + 1, PARTS - 1),)]
+    for group in order[:-1]:
+        for place, part in group:
+            arrive(place, part)
+        add(*group)
     incident_copy.wait()
     near_copy.wait()
-    arrive(*order[-1])
+    arrive(*order[-1][0])
     sums = []
     for chunk, at in enumerate(chunks):
-        total = running[at, :] + product(order[-1:], at)
-        for r in range(readers):
-            partial_value[r, at, :] = total[:, r * fields:(r + 1) * fields]
         for ahead in range(1, lags):
             other = lax.rem(lag + ahead, lags)
+            for j in range(own):
+                reader = other * own + j
+                theirs[ahead - 1, j, at] = running[reader, at] + product(
+                    order[-1], at, [reader]
+                )
             copy = pltpu.make_async_remote_copy(
-                src_ref=partial_value.at[pl.ds(other * own, own), pl.ds(chunk * rows, rows)],
+                src_ref=theirs.at[ahead - 1, :, pl.ds(chunk * rows, rows)],
                 dst_ref=landed.at[ahead - 1, :, pl.ds(chunk * rows, rows)],
                 send_sem=sum_send_sem.at[ahead - 1],
                 recv_sem=sum_recv_sem.at[ahead - 1, chunk],
@@ -421,37 +486,45 @@
             )
             copy.start()
             sums.append(copy)
+    for at in chunks:
+        for j in range(own):
+            reader = lag * own + j
+            mine[j, at] = incident[j, at].astype(jnp.float32) - (
+                running[reader, at] + product(order[-1], at, [reader])
+            )
     def parts_of(taken):
-        return blocks * len([part for part in range(PARTS) if taken(part)])
+        return subs * len([part for part in range(PARTS) if taken(part)])
 
     def when(condition, number):
         return jnp.where(condition, number, 0).astype(jnp.int32)
 
-    near_x, far_x = NEAR_BY_X * blocks, FAR_BY_X * blocks
-    ringed, at_once = RING_OWN * blocks, DIRECT * blocks
+    near_x, far_x = NEAR_BY_X * subs, FAR_BY_X * subs
+    ringed = parts_of(lambda part: part in RING)
+    ringed_far = parts_of(lambda part: part in RING_FAR)
     straight = parts_of(lambda part: part in STRAIGHT)
+    at_once = parts_of(lambda part: part in AT_ONCE)
+    handed = parts_of(lambda part: part in HANDED)
     extra = jnp.where(
         feeds_near,
         near_x
         + when(near_end, each - near_x)
-        + when(jnp.logical_not(first), each - near_x)
+        + when(near_aside, each - near_x)
         + when(jnp.logical_not(before_end), each - far_x)
         + when(end, ringed + straight),
         when(jnp.logical_not(first), far_x)
         + when(jnp.logical_not(end), each - far_x)
-        + when(end, far_x + each - straight - at_once)
+        + when(end, far_x + ringed_far + handed)
+        + when(start, ringed)
         + when(before_end, at_once),
     )
 
-    @pl.when(skips_z)
-    def _():
-        bulk(3 * each - ringed, 0, 0).wait_send()
-
-    @pl.when(jnp.logical_not(skips_z))
-    def _():
-        bulk(3 * each, 0, 0).wait_send()
-
-    for number in range(blocks, 3 * each, blocks):
+    kept_back = when(skips_z, ringed) + when(skips_far, ringed_far)
+    for number in sorted({0, ringed, ringed_far}):
+        @pl.when(kept_back == number)
+        def _():
+            bulk(3 * each - number, 0, 0).wait_send()
+
+    for number in range(subs, 3 * each, subs):
         @pl.when(extra == number)
         def _():
             bulk(number, 1, 0).wait_send()
@@ -461,16 +534,16 @@
         for copy in sums[chunk * (lags - 1):(chunk + 1) * (lags - 1)]:
             copy.wait_recv()
         for j in range(own):
-            summed = partial_value[lag * own + j, at]
+            remainder = mine[j, at]
             for ahead in range(1, lags):
-                summed = summed + landed[ahead - 1, j, at]
-            remainder = (incident[j, at].astype(jnp.float32) - summed).astype(jnp.bfloat16)
+                remainder = remainder - landed[ahead - 1, j, at]
+            remainder = remainder.astype(jnp.bfloat16)
             term = jnp.dot(near[j, :, at], remainder, preferred_element_type=jnp.float32)
             solved[j] = term if chunk == 0 else solved[j] + term
     for j in range(own):
         out_ref[j] = solved[j].astype(out_ref.dtype)
     for ahead in range(1, lags):
-        whole = partial_value.at[pl.ds(0, own)]
+        whole = theirs.at[ahead - 1]
         pltpu.make_async_remote_copy(
             src_ref=whole, dst_ref=whole,
             send_sem=sum_send_sem.at[ahead - 1], recv_sem=sum_recv_sem.at[ahead - 1, 0],
@@ -484,7 +557,8 @@
     count = weights.shape[2]
     own = incident.shape[0]
     piece = depth // PARTS
-    arrivals = PARTS * (2 * readers + 1) + 1 + readers * (
+    subs = readers * SPLIT
+    arrivals = PARTS * (2 * subs + 1) + 1 + subs * (
         2 * PARTS - min(NEAR_BY_X, FAR_BY_X) - FAR_BY_X
     )
     in_hbm = pl.BlockSpec(memory_space=pltpu.HBM)
@@ -504,12 +578,13 @@
         scratch_shapes=[
             *[pltpu.SMEM(operand.shape, operand.dtype) for operand in held[:2]],
             dma((2,)),
-            [pltpu.VMEM((TRANSIT + 1, readers, piece, fields), history.dtype)] * PARTS,
+            [pltpu.VMEM((TRANSIT + 1, subs, piece // SPLIT, fields), history.dtype)] * PARTS,
             pltpu.VMEM(weights.shape[2:], weights.dtype),
             pltpu.VMEM(near_inverse.shape, near_inverse.dtype),
             pltpu.VMEM(incident.shape, incident.dtype),
-            pltpu.VMEM((depth, readers * fields), jnp.float32),
             pltpu.VMEM((readers, depth, fields), jnp.float32),
+            pltpu.VMEM((lags - 1, own, depth, fields), jnp.float32),
+            pltpu.VMEM((own, depth, fields), jnp.float32),
             pltpu.VMEM((lags - 1, own, depth, fields), jnp.float32),
             dma((2,)),
             dma((arrivals,)),

time: 19.8 us -> 19.7 us (level); the launches traced: 19.7 us -> 19.3 us
  Pallas kernels: 18.4 us -> 18 us
    pallas_call x1, Pallas kernels: 18.4 us -> 18 us  [relayed(): pl.pallas_call(functools.partial(relay_kernel, panels, lags), out_shape=p...]
where the time goes in v4:
time: 19.7 us; the launch traced here: 19.3 us
  Pallas kernels  18 us (91%)
  local copies, waits for them, and re-layouts  0.66 us (3%)
  between operations  0.66 us (3%)
    pallas_call x1, Pallas kernels, relayed(): pl.pallas_call(functools.partial(relay_kernel, panels, lags), out_shape=p...  18 us
    unnamed x1, local copies, waits for them, and re-layouts  0.66 us

profile of v4, /device:TPU:1, one launch (start us, length us, event | category | flops | bytes accessed | tf_op | source)
XLA Modules:
  0.0 19.3 jit_solution(16301841451078842932)
XLA Ops:
  0.7 18.0 %shard_map.73 = bf16[1,512,128]{2,1,0:T(8,128)(2,1)S(1)} custom-call(s32[1,1]{1,0:T(1,128)S(6)} %copy.10.counts_ref, s32[1,3,1,6]{3,2,1,0:T(1,128)} %bitcast.3, s32[1,5,2,16]{3,2,1,0:T(2,128)} %bitcast.2, bf16[1,2,512,128]{3,2,1,0:T(8,128)(2,1)} %local_ref.1, bf16[1,1,6,512,512]{4,3,2,1,0:T(8,128)(2,1)} %weights_ref.1, bf16[1,512,128]{2,1,0:T(8,128)(2,1)} %incident_ref.1, ...), custom_call_target="tpu_custom_call" | custom-call | tf_op jit(solution)/shard_map/pallas_call | solution.py:573
  18.7 0.7 %copy.9 = bf16[1,512,128]{2,1,0:T(8,128)(2,1)} copy(bf16[1,512,128]{2,1,0:T(8,128)(2,1)S(1)} %shard_map.73) | data formatting | bytes 262144

commit v5 on v4

--- a/solution.py
+++ b/solution.py
@@ -18,6 +18,7 @@
 STRAIGHT = (1,)
 HANDED = (3,)
 RING_STEP = 5
+GIVE_STEP = 2
 DEFERRED = 2
 SPLIT = 1
 OWN, ACROSS, BESIDE, BEYOND, FOURTH, TRANSIT, LASTING = range(7)
@@ -33,7 +34,7 @@
     pairs_ref, send_ref, scalar_sem,
     windows, weights, near, incident, running, theirs, mine, landed,
     send_sem, recv_sem, local_sem, weight_sem, near_sem, incident_sem,
-    sum_send_sem, sum_recv_sem, chain_sem,
+    sum_send_sem, sum_recv_sem, chain_sem, give_sem,
 ):
     here = lax.axis_index("panel")
     lag = lax.axis_index("lag")
@@ -66,6 +67,10 @@
     skips_z = jnp.logical_and(before_end, feeds_far)
     skips_far = jnp.logical_and(before_end, feeds_near)
     start_far = jnp.logical_and(start, feeds_far)
+    gives = jnp.logical_and(waits_long, feeds_near)
+    takes = jnp.logical_and(jnp.logical_and(y == 0, at_chain == 1), feeds_near)
+    far_aside = jnp.logical_and(feeds_far, jnp.logical_not(jnp.logical_or(end, waits_long)))
+    far_over = jnp.logical_and(feeds_near, jnp.logical_not(jnp.logical_or(before_end, start)))
 
     def stays(part, block):
         skipped = here < 0
@@ -132,17 +137,26 @@
             greet(barrier, panel=panel(-3))
             greet(barrier, panel=panel(-1))
 
+    @pl.when(gives)
+    def _():
+        greet(barrier, panel=panel(1))
+
     for ahead in range(1, lags):
         greet(barrier, lag=lax.rem(lag + ahead, lags))
     pl.semaphore_wait(
         barrier,
         1
         + lags
+        + jnp.where(takes, 1, 0).astype(jnp.int32)
         + jnp.where(
             waits_long, 0,
             jnp.where(end, jnp.where(feeds_near, 3, 2), jnp.where(skips_z, 2, 1)),
         ).astype(jnp.int32),
     )
+    @pl.when(takes)
+    def _():
+        greet(give_sem, panel=panel(-1))
+
     pltpu.make_async_copy(local_ref.at[0], local_ref.at[0], local_sem).wait()
 
     pieces = [(part, sub) for part in range(PARTS) for sub in range(subs)]
@@ -373,6 +387,14 @@
                     for missed in deferred:
                         by_z(*missed).start()
 
+            if step == GIVE_STEP:
+                @pl.when(gives)
+                def _():
+                    pl.semaphore_wait(give_sem, 1)
+                    for given in pieces:
+                        if given[0] >= FAR_BY_X:
+                            fourth_straight(*given).start()
+
             if step == RING_STEP:
                 @pl.when(start_far)
                 def _():
@@ -399,7 +421,7 @@
                         fourth_by_y(part, block).start()
 
                 if part >= FAR_BY_X:
-                    @pl.when(feeds_far)
+                    @pl.when(far_aside)
                     def _():
                         fourth_by_y(part, block).start()
 
@@ -424,7 +446,7 @@
         if step == len(pieces) + ASIDE - 1:
             add(*[(ACROSS, part) for part in range(alone, PARTS)])
 
-    @pl.when(jnp.logical_and(feeds_near, jnp.logical_not(before_end)))
+    @pl.when(far_over)
     def _():
         for part, block in backward:
             if part >= FAR_BY_X:
@@ -509,10 +531,11 @@
         near_x
         + when(near_end, each - near_x)
         + when(near_aside, each - near_x)
-        + when(jnp.logical_not(before_end), each - far_x)
+        + when(far_over, each - far_x)
+        + when(gives, each - far_x)
         + when(end, ringed + straight),
         when(jnp.logical_not(first), far_x)
-        + when(jnp.logical_not(end), each - far_x)
+        + when(far_aside, each - far_x)
         + when(end, far_x + ringed_far + handed)
         + when(start, ringed)
         + when(before_end, at_once),
@@ -594,6 +617,7 @@
             dma,
             dma((lags - 1,)),
             dma((lags - 1, CHUNKS)),
+            pltpu.SemaphoreType.REGULAR,
             pltpu.SemaphoreType.REGULAR,
         ],
         compiler_params=pltpu.CompilerParams(

time: 19.7 us -> 19.7 us (level)
  no operation moved by 1% of the time
where the time goes in v5:
time: 19.7 us; the launch traced here: 19.3 us
  Pallas kernels  18 us (91%)
  local copies, waits for them, and re-layouts  0.66 us (3%)
  between operations  0.66 us (3%)
    pallas_call x1, Pallas kernels, relayed(): pl.pallas_call(functools.partial(relay_kernel, panels, lags), out_shape=p...  18 us
    unnamed x1, local copies, waits for them, and re-layouts  0.66 us

profile of v5, /device:TPU:1, one launch (start us, length us, event | category | flops | bytes accessed | tf_op | source)
XLA Modules:
  0.0 19.3 jit_solution(8095811912662893105)
XLA Ops:
  0.7 18.0 %shard_map.73 = bf16[1,512,128]{2,1,0:T(8,128)(2,1)S(1)} custom-call(s32[1,1]{1,0:T(1,128)S(6)} %copy.10.counts_ref, s32[1,3,1,6]{3,2,1,0:T(1,128)} %bitcast.3, s32[1,5,2,16]{3,2,1,0:T(2,128)} %bitcast.2, bf16[1,2,512,128]{3,2,1,0:T(8,128)(2,1)} %local_ref.1, bf16[1,1,6,512,512]{4,3,2,1,0:T(8,128)(2,1)} %weights_ref.1, bf16[1,512,128]{2,1,0:T(8,128)(2,1)} %incident_ref.1, ...), custom_call_target="tpu_custom_call" | custom-call | tf_op jit(solution)/shard_map/pallas_call | solution.py:596
  18.7 0.7 %copy.9 = bf16[1,512,128]{2,1,0:T(8,128)(2,1)} copy(bf16[1,512,128]{2,1,0:T(8,128)(2,1)S(1)} %shard_map.73) | data formatting | bytes 262144
